TPU v7x, 32 devices: a whole 2x2x4 slice. The times are simulated.
32 devices in a mesh: gx: 2 (over core), gy: 4 (over y, x), gz: 4 (over z).
Axes of the slice: x: 2, y: 2, z: 4, core: 2. Of those that a mesh axis runs over, the one named last changes fastest.
Arguments:
- displacement: float32 [3, 12, 24, 1536], P(None, 'gx', 'gy', 'gz'), may hold values from -0.18 to 0.18
- size_field_modes: float32 [27, 4, 8, 512], P(None, 'gx', 'gy', 'gz'), may hold values from -6 to 6
- velocity: float32 [3, 4, 8, 512], P(None, 'gx', 'gy', 'gz'), may hold values from -1 to 1
Outputs:
- advected_field: float32 [27, 4, 8, 512], P(None, 'gx', 'gy', 'gz')
- gradient: float32 [3, 12, 24, 1536], P(None, 'gx', 'gy', 'gz')
- checks: float32 [3], replicated
All inputs are finite; a program needn't handle non-finite values. Where the computation divides by a largest or mean magnitude, that divisor is 1e-20 or more.
Results may differ from a plain program's by a relative error of at most 0.0001.
Values sent between devices are 32-bit elements; how exact they have to be, the bound alone decides.
A program may use at most 64 MiB of HBM per device.

v0:
```python
import functools

import jax
import jax.numpy as jnp
import numpy as np
from jax import lax
from jax.experimental import pallas as pl
from jax.experimental.pallas import tpu as pltpu
from jax.sharding import PartitionSpec as P

SUBSTEPS = 4
MESH = pl.DeviceIdType.MESH
AXES = ("gx", "gy", "gz")

plus_values = (0.7071067811865476, 1.224744871391589, 1.5811388300841898)
g10 = 1.7320508075688772
g21 = 3.872983346207417
courant = 0.1
theta_size = 0.3
trial_step = 0.05


def tables_1d():
    points = np.array(
        [-0.8611363115940526, -0.3399810435848563, 0.3399810435848563, 0.8611363115940526]
    )
    weights = np.array(
        [0.3478548451374538, 0.6521451548625461, 0.6521451548625461, 0.3478548451374538]
    )
    points = 0.5 * (points + 1.0)
    weights = 0.5 * weights
    nodes = np.array([0.0, 1.0 / 3.0, 2.0 / 3.0, 1.0])
    value = np.zeros((4, 4))
    slope = np.zeros((4, 4))
    for m in range(4):
        others = [nodes[o] for o in range(4) if o != m]
        den = np.prod([nodes[m] - o for o in others])
        for q in range(4):
            g = points[q]
            value[q, m] = np.prod([g - o for o in others]) / den
            slope[q, m] = (
                sum(np.prod([g - others[t] for t in range(3) if t != s]) for s in range(3)) / den
            )
    c = 2.0 * points - 1.0
    legendre = np.stack(
        [
            np.full(4, plus_values[0]),
            plus_values[1] * c,
            plus_values[2] * 0.5 * (3.0 * c**2 - 1.0),
        ],
        axis=1,
    )
    return value, slope, legendre, weights


def row_tables(Y, Z):
    value, slope, legendre, weights = tables_1d()
    rows, nodes = 4 * Y, 3 * Y + 1
    tv = np.zeros((rows, rows))
    td = np.zeros((rows, rows))
    for e in range(Y):
        tv[4 * e : 4 * e + 4, 3 * e : 3 * e + 4] = value
        td[4 * e : 4 * e + 4, 3 * e : 3 * e + 4] = slope
    blocks = [tv[:, j] for j in range(nodes)] + [td[:, j] for j in range(nodes)]
    blocks += [tv[s, :] for s in range(rows)] + [td[s, :] for s in range(rows)]
    for b in range(3):
        for e in range(Y):
            col = np.zeros(rows)
            col[4 * e : 4 * e + 4] = legendre[:, b]
            blocks.append(col)
    blocks.append(np.tile(weights, Y))
    stacked = np.stack(blocks).astype(np.float32)
    return np.ascontiguousarray(np.broadcast_to(stacked[:, :, None], stacked.shape + (Z,)))


def kernel(sizes, X, Y, Z, disp, modes, vel, tab, adv, grad, checks,
           perm, slab, U, W, VEL, FS, SX, RX, SY, RY, SZ, RZ,
           RED, REDR, N, GN, A, G, B, SIZ,
           NXR, NYS, NYR, NZS, NZR, FXR, FYS, FYR, FZS, FZR,
           hs, hr, rs, rr, ns, nr, fs, fr):
    value, slope, legendre, weights = tables_1d()
    NX, NY = 3 * X, 3 * Y
    ROWS = 4 * Y
    EL = X * Y
    f32 = jnp.float32
    index = [lax.axis_index(a) for a in AXES]
    lane = lax.broadcasted_iota(jnp.int32, (ROWS, Z), 1)
    row = lax.broadcasted_iota(jnp.int32, (ROWS, Z), 0)
    oTV, oTD, oGV, oGD, oL, oW = 0, NY + 1, 2 * NY + 2, 2 * NY + 2 + ROWS, 2 * NY + 2 + 2 * ROWS, 2 * NY + 2 + 2 * ROWS + 3 * Y

    def at(axis, by):
        n = sizes[axis]
        return {AXES[axis]: lax.rem(index[axis] + (by + n), n)}

    barrier = pltpu.get_barrier_semaphore()
    total = 0
    for axis in range(3):
        for by in range(1, sizes[axis]):
            pl.semaphore_signal(barrier, inc=1, device_id=at(axis, by), device_id_type=MESH)
            total += 1

    def copy(src, dst, ss, sr, axis, by):
        return pltpu.make_async_remote_copy(
            src_ref=src, dst_ref=dst, send_sem=ss, recv_sem=sr,
            device_id=at(axis, by), device_id_type=MESH,
        )

    U[...] = jnp.zeros_like(U)
    VEL[...] = jnp.zeros_like(VEL)
    for ix in range(X):
        U[:, ix * Y : ix * Y + Y, :] = modes[:, ix]
        VEL[:, ix * Y : ix * Y + Y, :] = vel[:, ix]
    RED[0, 0] = jnp.zeros((2, ROWS, Z), f32)
    RED[0, 0, 0] = jnp.abs(VEL[0]) + jnp.abs(VEL[1]) + jnp.abs(VEL[2])
    a_i = lax.broadcasted_iota(jnp.int32, (3 * Z, 3 * Z), 0)
    b_i = lax.broadcasted_iota(jnp.int32, (3 * Z, 3 * Z), 1)
    b_k = (b_i >= Z).astype(jnp.int32) + (b_i >= 2 * Z).astype(jnp.int32)
    perm[...] = (a_i == 3 * (b_i - b_k * Z) + b_k).astype(f32)
    slab[...] = jnp.zeros_like(slab)
    for c in range(3):
        for i in range(NX):
            slab[c * NX + i, 0:NY, :] = disp[c, i]
    spread = jnp.dot(
        slab[...].reshape(3 * NX * ROWS, 3 * Z), perm[...],
        precision=lax.Precision.HIGHEST, preferred_element_type=f32,
    ).reshape(3, NX, ROWS, 3 * Z)
    for c in range(3):
        for k in range(3):
            N[c, 0:NX, k] = spread[c, :, :, k * Z : (k + 1) * Z]

    pl.semaphore_wait(barrier, total)

    def red_copies(r, axis):
        off = sum(sizes[t] - 1 for t in range(axis))
        return [
            copy(RED.at[r, axis], REDR.at[r, off + by - 1], rs.at[r, off + by - 1], rr.at[r, off + by - 1], axis, by)
            for by in range(1, sizes[axis])
        ]

    def red_start(r, axis):
        for cp in red_copies(r, axis):
            cp.start()

    def red_finish(r, axis, op):
        off = sum(sizes[t] - 1 for t in range(axis))
        for cp in red_copies(r, axis):
            cp.wait()
        total = RED[r, axis]
        for by in range(1, sizes[axis]):
            total = op(total, REDR[r, off + by - 1])
        RED[r, axis + 1] = total

    def rim_x(a, t):
        return copy(a.at[:, 0, 0:3], NXR.at[t], ns.at[t, 0], nr.at[t, 0], 0, -1)

    def rim_y(t):
        return copy(NYS.at[t], NYR.at[t], ns.at[t, 1], nr.at[t, 1], 1, -1)

    def rim_y_pack(a, t):
        for c in range(3):
            for k in range(3):
                a[c, NX, k] = NXR[t, c, k]
        for c in range(3):
            for i in range(NX + 1):
                for k in range(3):
                    NYS[t, c, i, k : k + 1, :] = a[c, i, k, 0:1, :]

    def rim_y_unpack(a, t):
        for c in range(3):
            for i in range(NX + 1):
                for k in range(3):
                    a[c, i, k, NY : NY + 1, :] = NYR[t, c, i, k : k + 1, :]

    def rim_z(t):
        return copy(NZS.at[t], NZR.at[t], ns.at[t, 2], nr.at[t, 2], 2, -1)

    def rim_z_pack(a, t):
        packed = jnp.zeros((ROWS, Z), f32)
        for c in range(3):
            for i in range(NX + 1):
                packed = jnp.where(lane == c * (NX + 1) + i, a[c, i, 0][:, 0:1], packed)
        NZS[t] = packed

    def rim_z_unpack(a, t):
        packed = NZR[t]
        for c in range(3):
            for i in range(NX + 1):
                at_ = c * (NX + 1) + i
                a[c, i, 3] = jnp.where(lane == Z - 1, packed[:, at_ : at_ + 1], pltpu.roll(a[c, i, 0], Z - 1, 1))

    def halo_copies(s):
        out = []
        for d, (sb, rb) in enumerate(((SX, RX), (SY, RY), (SZ, RZ))):
            for way in range(2):
                out.append(copy(sb.at[s, way], rb.at[s, way], hs.at[s, 2 * d + way], hr.at[s, 2 * d + way], d, 1 - 2 * way))
        return out

    def send_parts(s, n, tp, tm):
        SX[s, 0, n] = tp[0][(X - 1) * Y : EL]
        SX[s, 1, n] = tm[0][0:Y]
        for ix in range(X):
            SY[s, 0, n, ix : ix + 1] = tp[1][ix * Y + Y - 1 : ix * Y + Y]
            SY[s, 1, n, ix : ix + 1] = tm[1][ix * Y : ix * Y + 1]

    def prev_of(d, t, s, n):
        if d == 0:
            return jnp.concatenate([RX[s, 0, n], t[: ROWS - Y]], axis=0)
        if d == 1:
            parts = []
            for ix in range(X):
                parts += [RY[s, 0, n, ix : ix + 1], t[ix * Y : ix * Y + Y - 1]]
            return jnp.concatenate(parts + [t[EL:]], axis=0)
        return jnp.where(lane == 0, RZ[s, 0][:, n : n + 1], pltpu.roll(t, 1, 1))

    def next_of(d, t, s, n):
        if d == 0:
            return jnp.concatenate([t[Y:EL], RX[s, 1, n], t[EL:]], axis=0)
        if d == 1:
            parts = []
            for ix in range(X):
                parts += [t[ix * Y + 1 : ix * Y + Y], RY[s, 1, n, ix : ix + 1]]
            return jnp.concatenate(parts + [t[EL:]], axis=0)
        return jnp.where(lane == Z - 1, RZ[s, 1][:, n : n + 1], pltpu.roll(t, Z - 1, 1))

    strides = (9, 3, 1)
    others = [[m for m in range(27) if (m // strides[d]) % 3 == 0] for d in range(3)]

    def rate(src, s, first, between):
        u = [src[m] for m in range(27)]
        tp, tm = [[], [], []], [[], [], []]
        for d in range(3):
            for m in others[d]:
                even = plus_values[0] * u[m] + plus_values[2] * u[m + 2 * strides[d]]
                odd = plus_values[1] * u[m + strides[d]]
                tp[d].append(even + odd)
                tm[d].append(even - odd)
        up, low = jnp.zeros((ROWS, Z), f32), jnp.zeros((ROWS, Z), f32)
        for n in range(9):
            send_parts(s, n, [tp[d][n] for d in range(3)], [tm[d][n] for d in range(3)])
            up = jnp.where(lane == n, tp[2][n][:, Z - 1 : Z], up)
            low = jnp.where(lane == n, tm[2][n][:, 0:1], low)
        v = [VEL[d] for d in range(3)]
        send_parts(s, 9, v, v)
        if first:
            up = jnp.where(lane == 9, v[2][:, Z - 1 : Z], up)
            low = jnp.where(lane == 9, v[2][:, 0:1], low)
        SZ[s, 0] = up
        SZ[s, 1] = low
        for cp in halo_copies(s):
            cp.start()
        acc = [None] * 27
        for d in range(3):
            st = strides[d]
            va, vb = (2.0 * g10) * v[d], (2.0 * g21) * v[d]
            for m in others[d]:
                for mm, term in ((m + st, va * u[m]), (m + 2 * st, vb * u[m + st])):
                    acc[mm] = term if acc[mm] is None else acc[mm] + term
        between()
        for cp in halo_copies(s):
            cp.wait()
        if first:
            for d in range(3):
                high = v[d] + next_of(d, v[d], s, 9)
                lowf = prev_of(d, v[d], s, 9) + v[d]
                FS[d, 0] = jnp.maximum(high, 0.0)
                FS[d, 1] = jnp.minimum(high, 0.0)
                FS[d, 2] = jnp.maximum(lowf, 0.0)
                FS[d, 3] = jnp.minimum(lowf, 0.0)
        for d in range(3):
            st = strides[d]
            hp, hm, lp, lm = [FS[d, t] for t in range(4)]
            for n, m in enumerate(others[d]):
                hi = hp * tp[d][n] + hm * next_of(d, tm[d][n], s, n)
                lo = lp * prev_of(d, tp[d][n], s, n) + lm * tm[d][n]
                diff, both = lo - hi, lo + hi
                for mm, term in (
                    (m, plus_values[0] * diff),
                    (m + st, (-plus_values[1]) * both),
                    (m + 2 * st, plus_values[2] * diff),
                ):
                    acc[mm] = term if acc[mm] is None else acc[mm] + term
        return acc

    red_start(0, 0)
    rim_x(N, 0).start()

    def first_between():
        red_finish(0, 0, jnp.maximum)
        red_start(0, 1)
        rim_x(N, 0).wait()
        rim_y_pack(N, 0)
        rim_y(0).start()

    def second_between():
        red_finish(0, 1, jnp.maximum)
        red_start(0, 2)
        rim_y(0).wait()
        rim_y_unpack(N, 0)
        rim_z_pack(N, 0)
        rim_z(0).start()

    w1 = rate(U, 0, True, first_between)
    for m in range(27):
        W[m] = w1[m]
    w2 = rate(W, 1, False, second_between)
    red_finish(0, 2, jnp.maximum)
    rim_z(0).wait()
    rim_z_unpack(N, 0)
    fastest = jnp.max(RED[0, 3, 0], axis=(0, 1), keepdims=True)
    dt = courant / jnp.maximum(fastest, 0.25)
    dt = jnp.broadcast_to(dt, (ROWS, Z))
    half = 0.5 * dt * dt
    for m in range(27):
        U[m] = U[m] + dt * W[m] + half * w2[m]

    def substep(t, carry):
        w = rate(U, 2 * t, False, lambda: None)
        for m in range(27):
            W[m] = w[m]
        w = rate(W, 2 * t + 1, False, lambda: None)
        for m in range(27):
            U[m] = U[m] + dt * W[m] + half * w[m]
        return carry

    lax.fori_loop(1, SUBSTEPS, substep, 0)
    for ix in range(X):
        adv[:, ix] = U[:, ix * Y : ix * Y + Y, :]

    def size_of(ix, carry):
        mid = {}
        for a in range(3):
            for r in range(4):
                mid[a, r] = None
            for c in range(3):
                t = None
                for b in range(3):
                    for e in range(Y):
                        term = tab[oL + b * Y + e] * U[a * 9 + b * 3 + c, pl.ds(ix * Y + e, 1), :]
                        t = term if t is None else t + term
                for r in range(4):
                    term = float(legendre[r, c]) * t
                    mid[a, r] = term if mid[a, r] is None else mid[a, r] + term
        for p in range(4):
            for r in range(4):
                s = sum(float(legendre[p, a]) * mid[a, r] for a in range(3))
                SIZ[ix, p, r] = jnp.exp(theta_size * s)
        return carry

    lax.fori_loop(0, X, size_of, 0)

    def energy(with_grad):
        def yz(i, carry):
            for c in range(3):
                yv, yd = [], []
                for k in range(4):
                    sv = sd = None
                    for j in range(NY + 1):
                        x = N[c, i, k, j : j + 1, :]
                        tv, td = tab[oTV + j] * x, tab[oTD + j] * x
                        sv = tv if sv is None else sv + tv
                        sd = td if sd is None else sd + td
                    yv.append(sv)
                    yd.append(sd)
                for r in range(4):
                    A[0, c, i, r] = sum(float(value[r, k]) * yv[k] for k in range(4))
                    A[1, c, i, r] = sum(float(value[r, k]) * yd[k] for k in range(4))
                    A[2, c, i, r] = sum(float(slope[r, k]) * yv[k] for k in range(4))
            return carry

        lax.fori_loop(0, NX + 1, yz, 0)
        wrow = tab[oW]

        def gauss(t, esum):
            ix, r = t // 4, t % 4
            wr = jnp.where((r == 0) | (r == 3), float(weights[0]), float(weights[1]))
            for p in range(4):
                size = SIZ[ix, p, r]
                inv = 1.0 / size
                M = [[None] * 3 for _ in range(3)]
                for c in range(3):
                    for d in range(3):
                        tb = slope if d == 0 else value
                        jac = sum(float(tb[p, m]) * A[d, c, 3 * ix + m, r] for m in range(4))
                        if c == d:
                            jac = jac + 1.0
                        M[c][d] = jac * inv
                D = [[None] * 3 for _ in range(3)]
                metric = None
                for d in range(3):
                    for e in range(d, 3):
                        dev = M[0][d] * M[0][e] + M[1][d] * M[1][e] + M[2][d] * M[2][e]
                        if d == e:
                            dev = dev - 1.0
                        D[d][e] = D[e][d] = dev
                        sq = dev * dev
                        if d != e:
                            sq = 2.0 * sq
                        metric = sq if metric is None else metric + sq
                w = wrow * (wr * float(weights[p]))
                size2 = size * size
                esum = esum + w * (size2 * size) * metric
                if with_grad:
                    scale = (4.0 * w) * size2
                    for c in range(3):
                        for d in range(3):
                            g = M[c][0] * D[0][d] + M[c][1] * D[1][d] + M[c][2] * D[2][d]
                            G[d, c, ix, p, r] = scale * g
            return esum

        return lax.fori_loop(0, 4 * X, gauss, jnp.zeros((ROWS, Z), f32))

    esum = energy(True)

    def back_c(c, carry):
        for i in range(NX + 1):
            bv = [None] * 4
            bd = [None] * 4
            for r in range(4):
                ga = []
                for d in range(3):
                    tb = slope if d == 0 else value
                    acc = None
                    for ix in range(X):
                        m = i - 3 * ix
                        if 0 <= m <= 3:
                            for p in range(4):
                                term = float(tb[p, m]) * G[d, c, ix, p, r]
                                acc = term if acc is None else acc + term
                    ga.append(acc)
                for k in range(4):
                    tv = float(value[r, k]) * ga[0] + float(slope[r, k]) * ga[2]
                    td = float(value[r, k]) * ga[1]
                    bv[k] = tv if bv[k] is None else bv[k] + tv
                    bd[k] = td if bd[k] is None else bd[k] + td
            for k in range(4):
                B[0, i, k] = bv[k]
                B[1, i, k] = bd[k]
        for i in range(NX + 1):
            for k in range(4):
                acc = None
                for s in range(ROWS):
                    term = tab[oGV + s] * B[0, i, k, s : s + 1, :] + tab[oGD + s] * B[1, i, k, s : s + 1, :]
                    acc = term if acc is None else acc + term
                GN[c, i, k] = acc
        return carry

    lax.fori_loop(0, 3, back_c, 0)

    packed = jnp.zeros((ROWS, Z), f32)
    for c in range(3):
        for i in range(NX + 1):
            packed = jnp.where(lane == c * (NX + 1) + i, GN[c, i, 3][:, Z - 1 : Z], packed)
    FZS[...] = packed
    cz = copy(FZS, FZR, fs.at[0], fr.at[0], 2, 1)
    cz.start()
    cz.wait()
    packed = FZR[...]
    for c in range(3):
        for i in range(NX + 1):
            at_ = c * (NX + 1) + i
            GN[c, i, 0] = GN[c, i, 0] + jnp.where(lane == 0, packed[:, at_ : at_ + 1], pltpu.roll(GN[c, i, 3], 1, 1))
    cx = copy(GN.at[:, NX, 0:3], FXR, fs.at[1], fr.at[1], 0, 1)
    cx.start()
    cx.wait()
    for c in range(3):
        for k in range(3):
            GN[c, 0, k] = GN[c, 0, k] + FXR[c, k]
    for c in range(3):
        for i in range(NX):
            for k in range(3):
                FYS[c, i, k : k + 1, :] = GN[c, i, k, NY : NY + 1, :]
    cy = copy(FYS, FYR, fs.at[2], fr.at[2], 1, 1)
    cy.start()
    cy.wait()
    ssum = jnp.zeros((ROWS, Z), f32)
    for c in range(3):
        for i in range(NX):
            for k in range(3):
                GN[c, i, k, 0:1, :] = GN[c, i, k, 0:1, :] + FYR[c, i, k : k + 1, :]
    for c in range(3):
        for i in range(NX):
            for k in range(3):
                g = GN[c, i, k]
                ssum = ssum + g * g
    ssum = jnp.where(row < NY, ssum, 0.0)
    RED[1, 0, 0] = esum
    RED[1, 0, 1] = ssum
    red_start(1, 0)
    rim_x(GN, 1).start()
    red_finish(1, 0, jnp.add)
    red_start(1, 1)
    rim_x(GN, 1).wait()
    rim_y_pack(GN, 1)
    rim_y(1).start()
    for c in range(3):
        for k in range(3):
            slab[c * NX : (c + 1) * NX, :, k * Z : (k + 1) * Z] = GN[c, 0:NX, k]
    woven = lax.dot_general(
        slab[...].reshape(3 * NX * ROWS, 3 * Z), perm[...], (((1,), (1,)), ((), ())),
        precision=lax.Precision.HIGHEST, preferred_element_type=f32,
    ).reshape(3, NX, ROWS, 3 * Z)
    grad[...] = woven[:, :, 0:NY, :]
    red_finish(1, 1, jnp.add)
    red_start(1, 2)
    rim_y(1).wait()
    rim_y_unpack(GN, 1)
    rim_z_pack(GN, 1)
    rim_z(1).start()
    red_finish(1, 2, jnp.add)
    devices = sizes[0] * sizes[1] * sizes[2]
    elements = float(EL * Z * devices)
    entries = 81.0 * elements
    etot = jnp.sum(RED[1, 3, 0], axis=(0, 1), keepdims=True)
    stot = jnp.sum(RED[1, 3, 1], axis=(0, 1), keepdims=True)
    step = jnp.broadcast_to(trial_step / jnp.sqrt(1.0 + stot / entries), (ROWS, Z))
    rim_z(1).wait()
    rim_z_unpack(GN, 1)
    for c in range(3):
        for i in range(NX + 1):
            for k in range(4):
                N[c, i, k] = N[c, i, k] - step * GN[c, i, k]
    tsum = energy(False)
    RED[2, 0, 0] = tsum
    RED[2, 0, 1] = jnp.zeros((ROWS, Z), f32)
    for axis in range(3):
        red_start(2, axis)
        red_finish(2, axis, jnp.add)
    ttot = jnp.sum(RED[2, 3, 0], axis=(0, 1), keepdims=True)
    l1 = lax.broadcasted_iota(jnp.int32, (1, Z), 1)
    checks[...] = jnp.where(
        l1 == 0, etot / elements, jnp.where(l1 == 1, stot / entries, ttot / elements)
    )


def solution(mesh):
    sizes = tuple(mesh.shape[a] for a in AXES)

    def on_device(displacement, size_field_modes, velocity):
        modes, X, Y, Z = size_field_modes.shape
        assert Y == 2 and displacement.shape == (3, 3 * X, 3 * Y, 3 * Z)
        R, NX, NY = 4 * Y, 3 * X, 3 * Y
        tab = jnp.asarray(row_tables(Y, Z))
        peers = sum(sizes) - 3
        S = 2 * SUBSTEPS
        vm = lambda *shape: pltpu.VMEM(shape, jnp.float32)
        dma = lambda *shape: pltpu.SemaphoreType.DMA(shape)
        spec = pl.BlockSpec(memory_space=pltpu.VMEM)
        adv, grad, checks = pl.pallas_call(
            functools.partial(kernel, sizes, X, Y, Z),
            out_shape=(
                jax.ShapeDtypeStruct(size_field_modes.shape, jnp.float32),
                jax.ShapeDtypeStruct(displacement.shape, jnp.float32),
                jax.ShapeDtypeStruct((1, Z), jnp.float32),
            ),
            in_specs=[spec] * 4,
            out_specs=(spec,) * 3,
            scratch_shapes=[
                vm(3 * Z, 3 * Z), vm(3 * NX, R, 3 * Z), vm(27, R, Z), vm(27, R, Z), vm(3, R, Z), vm(3, 4, R, Z),
                vm(S, 2, 10, Y, Z), vm(S, 2, 10, Y, Z), vm(S, 2, 10, X, Z), vm(S, 2, 10, X, Z),
                vm(S, 2, R, Z), vm(S, 2, R, Z),
                vm(3, 4, 2, R, Z), vm(3, peers, 2, R, Z),
                vm(3, NX + 1, 4, R, Z), vm(3, NX + 1, 4, R, Z),
                vm(3, 3, NX + 1, 4, R, Z), vm(3, 3, X, 4, 4, R, Z), vm(2, NX + 1, 4, R, Z), vm(X, 4, 4, R, Z),
                vm(2, 3, 3, R, Z), vm(2, 3, NX + 1, 3, Z), vm(2, 3, NX + 1, 3, Z), vm(2, R, Z), vm(2, R, Z),
                vm(3, 3, R, Z), vm(3, NX, 3, Z), vm(3, NX, 3, Z), vm(R, Z), vm(R, Z),
                dma(S, 6), dma(S, 6), dma(3, peers), dma(3, peers), dma(2, 3), dma(2, 3), dma(3), dma(3),
            ],
            compiler_params=pltpu.CompilerParams(collective_id=0, has_side_effects=True),
        )(displacement, size_field_modes, velocity, tab)
        return adv, grad, checks[0, 0:3]

    return jax.shard_map(
        on_device,
        mesh=mesh,
        in_specs=(P(None, "gx", "gy", "gz"),) * 3,
        out_specs=(P(None, "gx", "gy", "gz"), P(None, "gx", "gy", "gz"), P()),
        check_vma=False,
    )
```

profile of v0, /device:TPU:0, one launch (start us, length us, event | category | flops | bytes accessed | tf_op | source)
XLA Modules:
  0.0 71.8 jit_solution(18224481640660625895)
XLA Ops:
  0.6 66.9 %shard_map.67 = (f32[27,2,2,128]{3,2,1,0:T(2,128)}, f32[3,6,6,384]{3,2,1,0:T(8,128)}, f32[1,128]{1,0:T(1,128)}) custom-call(f32[3,6,6,384]{3,2,1,0:T(8,128)} %disp.1, f32[27,2,2,128]{3,2,1,0:T(2,128)} %modes.1, f32[3,2,2,128]{3,2,1,0:T(2,128)} %vel.1, f32[37,8,128]{2,1,0:T(8,128)} %constant.2.clone.tab), custom_call_target="tpu_custom_call" | custom-call | tf_op jit(solution)/shard_map/pallas_call | solution.py:548
  67.6 0.0 copy-start
  67.6 0.7 copy-done
  68.2 0.5 slice_bitcast_fusion
  68.8 1.4 %copy.9 = f32[27,2,2,128]{3,2,1,0:T(2,128)} copy(f32[27,2,2,128]{3,2,1,0:T(2,128)} %get-tuple-element.12) | data formatting | bytes 110592
  70.2 1.6 %copy.10 = f32[3,6,6,384]{3,2,1,0:T(8,128)} copy(f32[3,6,6,384]{3,2,1,0:T(8,128)} %get-tuple-element.13) | data formatting | bytes 331776
Async XLA Ops:
  67.6 0.7 copy-start
where the time goes:
time: 72.1 us; the launch traced here: 71.8 us
  Pallas kernels  66.9 us (93%)
  local copies, waits for them, and re-layouts  4.25 us (6%)
    pallas_call x1, Pallas kernels, on_device(): pl.pallas_call(functools.partial(kernel, sizes, X, Y, Z), out_shape=(jax....  66.9 us
    unnamed x4, local copies, waits for them, and re-layouts  3.74 us

commit v1 on v0

v1 whole, which is shorter than its diff:
```python
import functools

import jax
import jax.numpy as jnp
import numpy as np
from jax import lax
from jax.experimental import pallas as pl
from jax.experimental.pallas import tpu as pltpu
from jax.sharding import PartitionSpec as P

SUBSTEPS = 4
MESH = pl.DeviceIdType.MESH
AXES = ("gx", "gy", "gz")

plus_values = (0.7071067811865476, 1.224744871391589, 1.5811388300841898)
g10 = 1.7320508075688772
g21 = 3.872983346207417
courant = 0.1
theta_size = 0.3
trial_step = 0.05


def tables_1d():
    points = np.array(
        [-0.8611363115940526, -0.3399810435848563, 0.3399810435848563, 0.8611363115940526]
    )
    weights = np.array(
        [0.3478548451374538, 0.6521451548625461, 0.6521451548625461, 0.3478548451374538]
    )
    points = 0.5 * (points + 1.0)
    weights = 0.5 * weights
    nodes = np.array([0.0, 1.0 / 3.0, 2.0 / 3.0, 1.0])
    value = np.zeros((4, 4))
    slope = np.zeros((4, 4))
    for m in range(4):
        others = [nodes[o] for o in range(4) if o != m]
        den = np.prod([nodes[m] - o for o in others])
        for q in range(4):
            g = points[q]
            value[q, m] = np.prod([g - o for o in others]) / den
            slope[q, m] = (
                sum(np.prod([g - others[t] for t in range(3) if t != s]) for s in range(3)) / den
            )
    c = 2.0 * points - 1.0
    legendre = np.stack(
        [
            np.full(4, plus_values[0]),
            plus_values[1] * c,
            plus_values[2] * 0.5 * (3.0 * c**2 - 1.0),
        ],
        axis=1,
    )
    return value, slope, legendre, weights


def row_tables(Y, Z):
    value, slope, legendre, weights = tables_1d()
    rows, nodes = 4 * Y, 3 * Y + 1
    tv = np.zeros((rows, rows))
    td = np.zeros((rows, rows))
    for e in range(Y):
        tv[4 * e : 4 * e + 4, 3 * e : 3 * e + 4] = value
        td[4 * e : 4 * e + 4, 3 * e : 3 * e + 4] = slope
    blocks = [tv[:, j] for j in range(nodes)] + [td[:, j] for j in range(nodes)]
    blocks += [tv[s, :] for s in range(rows)] + [td[s, :] for s in range(rows)]
    for b in range(3):
        for e in range(Y):
            col = np.zeros(rows)
            col[4 * e : 4 * e + 4] = legendre[:, b]
            blocks.append(col)
    blocks.append(np.tile(weights, Y))
    stacked = np.stack(blocks).astype(np.float32)
    return np.ascontiguousarray(np.broadcast_to(stacked[:, :, None], stacked.shape + (Z,)))


def kernel(sizes, X, Y, Z, disp, modes, vel, tab, adv, grad, checks,
           perm, slab, U, W, VEL, FS, SX, RX, SY, RY, SZ, RZ,
           RED, REDR, N, GN, A, G, J, B, SIZ, DT,
           NXR, NYS, NYR, NZS, NZR, FXR, FYS, FYR, FZS, FZR,
           hs, hr, rs, rr, ns, nr, fs, fr):
    value, slope, legendre, weights = tables_1d()
    NX, NY = 3 * X, 3 * Y
    ROWS = 4 * Y
    EL = X * Y
    f32 = jnp.float32
    index = [lax.axis_index(a) for a in AXES]
    lane = lax.broadcasted_iota(jnp.int32, (ROWS, Z), 1)
    row = lax.broadcasted_iota(jnp.int32, (ROWS, Z), 0)
    oTV, oTD, oGV, oGD, oL, oW = 0, NY + 1, 2 * NY + 2, 2 * NY + 2 + ROWS, 2 * NY + 2 + 2 * ROWS, 2 * NY + 2 + 2 * ROWS + 3 * Y

    def at(axis, by):
        n = sizes[axis]
        return {AXES[axis]: lax.rem(index[axis] + (by + n), n)}

    barrier = pltpu.get_barrier_semaphore()
    total = 0
    moves = [(by, 0, 0) for by in range(1, sizes[0])]
    moves += [(0, b, c) for b in range(sizes[1]) for c in range(sizes[2]) if b or c]
    for move in moves:
        target = {}
        for axis in range(3):
            if move[axis]:
                target.update(at(axis, move[axis]))
        pl.semaphore_signal(barrier, inc=1, device_id=target, device_id_type=MESH)
        total += 1

    def copy(src, dst, ss, sr, axis, by):
        return pltpu.make_async_remote_copy(
            src_ref=src, dst_ref=dst, send_sem=ss, recv_sem=sr,
            device_id=at(axis, by), device_id_type=MESH,
        )

    U[...] = jnp.zeros_like(U)
    VEL[...] = jnp.zeros_like(VEL)
    for ix in range(X):
        U[:, ix * Y : ix * Y + Y, :] = modes[:, ix]
        VEL[:, ix * Y : ix * Y + Y, :] = vel[:, ix]
    RED[0, 0] = jnp.zeros_like(RED[0, 0])
    RED[0, 0, 0] = jnp.abs(VEL[0]) + jnp.abs(VEL[1]) + jnp.abs(VEL[2])
    def unweave():
        a_i = lax.broadcasted_iota(jnp.int32, (3 * Z, 3 * Z), 0)
        b_i = lax.broadcasted_iota(jnp.int32, (3 * Z, 3 * Z), 1)
        b_k = (b_i >= Z).astype(jnp.int32) + (b_i >= 2 * Z).astype(jnp.int32)
        perm[...] = (a_i == 3 * (b_i - b_k * Z) + b_k).astype(f32)
        slab[...] = jnp.zeros_like(slab)
        for c in range(3):
            for i in range(NX):
                slab[c * NX + i, 0:NY, :] = disp[c, i]
        spread = jnp.dot(
            slab[...].reshape(3 * NX * ROWS, 3 * Z), perm[...],
            precision=lax.Precision.HIGHEST, preferred_element_type=f32,
        ).reshape(3, NX, ROWS, 3 * Z)
        for c in range(3):
            for k in range(3):
                N[c, 0:NX, k] = spread[c, :, :, k * Z : (k + 1) * Z]

    pl.semaphore_wait(barrier, total)

    def peers_of(phase):
        if phase == 0:
            return [(by, 0, 0) for by in range(1, sizes[0])]
        return [(0, b, c) for b in range(sizes[1]) for c in range(sizes[2]) if b or c]

    def red_copies(r, phase):
        off = 0 if phase == 0 else sizes[0] - 1
        out = []
        for n, move in enumerate(peers_of(phase)):
            target = {}
            for axis in range(3):
                if move[axis]:
                    target.update(at(axis, move[axis]))
            out.append(pltpu.make_async_remote_copy(
                src_ref=RED.at[r, phase], dst_ref=REDR.at[r, off + n],
                send_sem=rs.at[r, off + n], recv_sem=rr.at[r, off + n],
                device_id=target, device_id_type=MESH,
            ))
        return out

    def red_start(r, phase):
        for cp in red_copies(r, phase):
            cp.start()

    def red_finish(r, phase, op):
        off = 0 if phase == 0 else sizes[0] - 1
        copies = red_copies(r, phase)
        for cp in copies:
            cp.wait()
        total = RED[r, phase]
        for n in range(len(copies)):
            total = op(total, REDR[r, off + n])
        RED[r, phase + 1] = total

    def rim_x(a, t):
        return copy(a.at[:, 0, 0:3], NXR.at[t], ns.at[t, 0], nr.at[t, 0], 0, -1)

    def rim_y(t):
        return copy(NYS.at[t], NYR.at[t], ns.at[t, 1], nr.at[t, 1], 1, -1)

    def rim_y_pack(a, t):
        for c in range(3):
            for k in range(3):
                a[c, NX, k] = NXR[t, c, k]
        for c in range(3):
            for i in range(NX + 1):
                for k in range(3):
                    NYS[t, c, i, k : k + 1, :] = a[c, i, k, 0:1, :]

    def rim_y_unpack(a, t):
        for c in range(3):
            for i in range(NX + 1):
                for k in range(3):
                    a[c, i, k, NY : NY + 1, :] = NYR[t, c, i, k : k + 1, :]

    def rim_z(t):
        return copy(NZS.at[t], NZR.at[t], ns.at[t, 2], nr.at[t, 2], 2, -1)

    def rim_z_pack(a, t):
        packed = jnp.zeros((ROWS, Z), f32)
        for c in range(3):
            for i in range(NX + 1):
                packed = jnp.where(lane == c * (NX + 1) + i, a[c, i, 0][:, 0:1], packed)
        NZS[t] = packed

    def rim_z_unpack(a, t):
        packed = NZR[t]
        for c in range(3):
            for i in range(NX + 1):
                at_ = c * (NX + 1) + i
                a[c, i, 3] = jnp.where(lane == Z - 1, packed[:, at_ : at_ + 1], pltpu.roll(a[c, i, 0], Z - 1, 1))

    def halo_copies(s, dims):
        out = []
        for d, (sb, rb) in ((0, (SX, RX)), (1, (SY, RY)), (2, (SZ, RZ))):
            if d not in dims:
                continue
            for way in range(2):
                out.append(copy(sb.at[s, way], rb.at[s, way], hs.at[s, 2 * d + way], hr.at[s, 2 * d + way], d, 1 - 2 * way))
        return out

    def send_part(s, n, d, tp, tm):
        if d == 0:
            SX[s, 0, n] = tp[(X - 1) * Y : EL]
            SX[s, 1, n] = tm[0:Y]
        else:
            for ix in range(X):
                SY[s, 0, n, ix : ix + 1] = tp[ix * Y + Y - 1 : ix * Y + Y]
                SY[s, 1, n, ix : ix + 1] = tm[ix * Y : ix * Y + 1]

    def prev_of(d, t, s, n):
        if d == 0:
            return jnp.concatenate([RX[s, 0, n], t[: ROWS - Y]], axis=0)
        if d == 1:
            parts = []
            for ix in range(X):
                parts += [RY[s, 0, n, ix : ix + 1], t[ix * Y : ix * Y + Y - 1]]
            return jnp.concatenate(parts + [t[EL:]], axis=0)
        return jnp.where(lane == 0, RZ[s, 0][:, n : n + 1], pltpu.roll(t, 1, 1))

    def next_of(d, t, s, n):
        if d == 0:
            return jnp.concatenate([t[Y:EL], RX[s, 1, n], t[EL:]], axis=0)
        if d == 1:
            parts = []
            for ix in range(X):
                parts += [t[ix * Y + 1 : ix * Y + Y], RY[s, 1, n, ix : ix + 1]]
            return jnp.concatenate(parts + [t[EL:]], axis=0)
        return jnp.where(lane == Z - 1, RZ[s, 1][:, n : n + 1], pltpu.roll(t, Z - 1, 1))

    strides = (9, 3, 1)
    others = [[m for m in range(27) if (m // strides[d]) % 3 == 0] for d in range(3)]

    def rate(src, s, first, between):
        u = [src[m] for m in range(27)]
        v = [VEL[d] for d in range(3)]
        tp, tm = [[], [], []], [[], [], []]
        for d in (2, 1, 0):
            for m in others[d]:
                even = plus_values[0] * u[m] + plus_values[2] * u[m + 2 * strides[d]]
                odd = plus_values[1] * u[m + strides[d]]
                tp[d].append(even + odd)
                tm[d].append(even - odd)
            ups = tp[d] + [v[d]]
            lows = tm[d] + [v[d]]
            if d == 2:
                up, low = jnp.zeros((ROWS, Z), f32), jnp.zeros((ROWS, Z), f32)
                for n in range(10 if first else 9):
                    up = jnp.where(lane == n, ups[n][:, Z - 1 : Z], up)
                    low = jnp.where(lane == n, lows[n][:, 0:1], low)
                SZ[s, 0] = up
                SZ[s, 1] = low
            else:
                for n in range(10):
                    send_part(s, n, d, ups[n], lows[n])
            for cp in halo_copies(s, (d,)):
                cp.start()
        acc = [None] * 27
        for d in range(3):
            st = strides[d]
            va, vb = (2.0 * g10) * v[d], (2.0 * g21) * v[d]
            for m in others[d]:
                for mm, term in ((m + st, va * u[m]), (m + 2 * st, vb * u[m + st])):
                    acc[mm] = term if acc[mm] is None else acc[mm] + term
        between()
        for d in range(3):
            for cp in halo_copies(s, (d,)):
                cp.wait()
            if first:
                high = v[d] + next_of(d, v[d], s, 9)
                lowf = prev_of(d, v[d], s, 9) + v[d]
                FS[d, 0] = jnp.maximum(high, 0.0)
                FS[d, 1] = jnp.minimum(high, 0.0)
                FS[d, 2] = jnp.maximum(lowf, 0.0)
                FS[d, 3] = jnp.minimum(lowf, 0.0)
            st = strides[d]
            hp, hm, lp, lm = [FS[d, t] for t in range(4)]
            for n, m in enumerate(others[d]):
                hi = hp * tp[d][n] + hm * next_of(d, tm[d][n], s, n)
                lo = lp * prev_of(d, tp[d][n], s, n) + lm * tm[d][n]
                diff, both = lo - hi, lo + hi
                for mm, term in (
                    (m, plus_values[0] * diff),
                    (m + st, (-plus_values[1]) * both),
                    (m + 2 * st, plus_values[2] * diff),
                ):
                    acc[mm] = term if acc[mm] is None else acc[mm] + term
        return acc

    def yz_of(src):
        def yz(i, carry):
            for c in range(3):
                yv, yd = [], []
                for k in range(4):
                    sv = sd = None
                    for j in range(NY + 1):
                        x = src[c, i, k, j : j + 1, :]
                        tv, td = tab[oTV + j] * x, tab[oTD + j] * x
                        sv = tv if sv is None else sv + tv
                        sd = td if sd is None else sd + td
                    yv.append(sv)
                    yd.append(sd)
                for r in range(4):
                    A[0, c, i, r] = sum(float(value[r, k]) * yv[k] for k in range(4))
                    A[1, c, i, r] = sum(float(value[r, k]) * yd[k] for k in range(4))
                    A[2, c, i, r] = sum(float(slope[r, k]) * yv[k] for k in range(4))
            return carry

        lax.fori_loop(0, NX + 1, yz, 0)

    def slope_at(ix, p, r, c, d):
        tb = slope if d == 0 else value
        return sum(float(tb[p, m]) * A[d, c, 3 * ix + m, r] for m in range(4))

    def jacobians(t):
        ix, r = t // 4, t % 4
        for p in range(4):
            for c in range(3):
                for d in range(3):
                    jac = slope_at(ix, p, r, c, d)
                    J[d, c, ix, p, r] = jac + 1.0 if c == d else jac

    red_start(0, 0)

    def between_0():
        red_finish(0, 0, jnp.maximum)
        red_start(0, 1)
        unweave()
        rim_x(N, 0).start()

    def between_1():
        rim_x(N, 0).wait()
        rim_y_pack(N, 0)
        rim_y(0).start()
        red_finish(0, 1, jnp.maximum)

    def between_2():
        rim_y(0).wait()
        rim_y_unpack(N, 0)
        rim_z_pack(N, 0)
        rim_z(0).start()

    def between_3():
        rim_z(0).wait()
        rim_z_unpack(N, 0)
        yz_of(N)

    def two_stages(s, first, between_a, between_b, dt_of):
        w = rate(U, s, first, between_a)
        for m in range(27):
            W[m] = w[m]
        w = rate(W, s + 1, False, between_b)
        dt = dt_of()
        half = 0.5 * dt * dt
        for m in range(27):
            U[m] = U[m] + dt * W[m] + half * w[m]

    def time_step():
        fastest = jnp.max(RED[0, 2, 0], axis=(0, 1), keepdims=True)
        DT[...] = jnp.broadcast_to(courant / jnp.maximum(fastest, 0.25), (ROWS, Z))
        return DT[...]

    two_stages(0, True, between_0, between_1, time_step)
    two_stages(2, False, between_2, between_3, lambda: DT[...])
    units = (4 * X) // (2 * SUBSTEPS - 4)

    def substep(t, carry):
        def some(s):
            def run():
                for n in range(units):
                    jacobians((s - 4) * units + n)
            return run

        two_stages(2 * t, False, some(2 * t), some(2 * t + 1), lambda: DT[...])
        return carry

    lax.fori_loop(2, SUBSTEPS, substep, 0)
    def size_of(ix, carry):
        mid = {}
        for a in range(3):
            for r in range(4):
                mid[a, r] = None
            for c in range(3):
                t = None
                for b in range(3):
                    for e in range(Y):
                        term = tab[oL + b * Y + e] * U[a * 9 + b * 3 + c, pl.ds(ix * Y + e, 1), :]
                        t = term if t is None else t + term
                for r in range(4):
                    term = float(legendre[r, c]) * t
                    mid[a, r] = term if mid[a, r] is None else mid[a, r] + term
        for p in range(4):
            for r in range(4):
                s = sum(float(legendre[p, a]) * mid[a, r] for a in range(3))
                SIZ[ix, p, r] = jnp.exp(theta_size * s)
        return carry

    lax.fori_loop(0, X, size_of, 0)

    wrow = tab[oW]
    pairs = [(d, e) for d in range(3) for e in range(d, 3)]

    def dot3(p, q, d, e):
        return p[0][d] * q[0][e] + p[1][d] * q[1][e] + p[2][d] * q[2][e]

    def gauss_weight(r):
        return jnp.where((r == 0) | (r == 3), float(weights[0]), float(weights[1]))

    def gauss(t, esum):
        ix, r = t // 4, t % 4
        for p in range(4):
            size = SIZ[ix, p, r]
            inv = 1.0 / size
            M = [[J[d, c, ix, p, r] * inv for d in range(3)] for c in range(3)]
            D = [[None] * 3 for _ in range(3)]
            metric = None
            for d, e in pairs:
                dev = dot3(M, M, d, e)
                if d == e:
                    dev = dev - 1.0
                D[d][e] = D[e][d] = dev
                sq = dev * dev if d == e else 2.0 * (dev * dev)
                metric = sq if metric is None else metric + sq
            w = wrow * (gauss_weight(r) * float(weights[p]))
            size2 = size * size
            esum = esum + w * (size2 * size) * metric
            scale = (4.0 * w) * size2
            for c in range(3):
                for d in range(3):
                    g = M[c][0] * D[0][d] + M[c][1] * D[1][d] + M[c][2] * D[2][d]
                    G[d, c, ix, p, r] = scale * g
        return esum

    zero = jnp.zeros((ROWS, Z), f32)
    esum = lax.fori_loop(0, 4 * X, gauss, zero)

    def back_c(c, carry):
        for i in range(NX + 1):
            bv = [None] * 4
            bd = [None] * 4
            for r in range(4):
                ga = []
                for d in range(3):
                    tb = slope if d == 0 else value
                    acc = None
                    for ix in range(X):
                        m = i - 3 * ix
                        if 0 <= m <= 3:
                            for p in range(4):
                                term = float(tb[p, m]) * G[d, c, ix, p, r]
                                acc = term if acc is None else acc + term
                    ga.append(acc)
                for k in range(4):
                    tv = float(value[r, k]) * ga[0] + float(slope[r, k]) * ga[2]
                    td = float(value[r, k]) * ga[1]
                    bv[k] = tv if bv[k] is None else bv[k] + tv
                    bd[k] = td if bd[k] is None else bd[k] + td
            for k in range(4):
                B[0, i, k] = bv[k]
                B[1, i, k] = bd[k]
        for i in range(NX + 1):
            for k in range(4):
                acc = None
                for s in range(ROWS):
                    term = tab[oGV + s] * B[0, i, k, s : s + 1, :] + tab[oGD + s] * B[1, i, k, s : s + 1, :]
                    acc = term if acc is None else acc + term
                GN[c, i, k] = acc
        return carry

    lax.fori_loop(0, 3, back_c, 0)

    def both_ways(src_up, src_down, axis, slot, up, down):
        copies = [
            copy(src_up, up, fs.at[slot], fr.at[slot], axis, 1),
            copy(src_down, down, fs.at[slot + 1], fr.at[slot + 1], axis, -1),
        ]
        for cp in copies:
            cp.start()
        for cp in copies:
            cp.wait()

    up, down = zero, zero
    for c in range(3):
        for i in range(NX + 1):
            here = lane == c * (NX + 1) + i
            up = jnp.where(here, GN[c, i, 3][:, Z - 1 : Z], up)
            down = jnp.where(here, GN[c, i, 0][:, 0:1], down)
    FZS[0] = up
    FZS[1] = down
    both_ways(FZS.at[0], FZS.at[1], 2, 0, FZR.at[0], FZR.at[1])
    up, down = FZR[0], FZR[1]
    for c in range(3):
        for i in range(NX + 1):
            n = c * (NX + 1) + i
            g0, g3 = GN[c, i, 0], GN[c, i, 3]
            full = g0 + jnp.where(lane == 0, up[:, n : n + 1], pltpu.roll(g3, 1, 1))
            GN[c, i, 0] = full
            GN[c, i, 3] = jnp.where(lane == Z - 1, g3 + down[:, n : n + 1], pltpu.roll(full, Z - 1, 1))
    both_ways(GN.at[:, NX], GN.at[:, 0], 0, 2, FXR.at[0], FXR.at[1])
    for c in range(3):
        for k in range(4):
            GN[c, 0, k] = GN[c, 0, k] + FXR[0, c, k]
            GN[c, NX, k] = GN[c, NX, k] + FXR[1, c, k]
    for c in range(3):
        for i in range(NX + 1):
            for k in range(4):
                FYS[0, c, i, k : k + 1, :] = GN[c, i, k, NY : NY + 1, :]
                FYS[1, c, i, k : k + 1, :] = GN[c, i, k, 0:1, :]
    both_ways(FYS.at[0], FYS.at[1], 1, 4, FYR.at[0], FYR.at[1])
    for c in range(3):
        for i in range(NX + 1):
            for k in range(4):
                GN[c, i, k, 0:1, :] = GN[c, i, k, 0:1, :] + FYR[0, c, i, k : k + 1, :]
                GN[c, i, k, NY : NY + 1, :] = GN[c, i, k, NY : NY + 1, :] + FYR[1, c, i, k : k + 1, :]
    ssum = zero
    for c in range(3):
        for i in range(NX):
            for k in range(3):
                g = GN[c, i, k]
                ssum = ssum + g * g
    ssum = jnp.where(row < NY, ssum, 0.0)
    devices = sizes[0] * sizes[1] * sizes[2]
    elements = float(EL * Z * devices)
    entries = 81.0 * elements
    mine = jnp.sum(ssum, axis=(0, 1), keepdims=True)
    bound = trial_step / jnp.sqrt(1.0 + mine / entries)
    bound = jnp.broadcast_to(bound, (ROWS, Z))
    yz_of(GN)

    def trial(t, sums):
        ix, r = t // 4, t % 4
        s1, s2, s3, s4 = sums
        for p in range(4):
            size = SIZ[ix, p, r]
            inv = 1.0 / size
            move = -(inv * bound)
            M = [[J[d, c, ix, p, r] * inv for d in range(3)] for c in range(3)]
            K = [[slope_at(ix, p, r, c, d) * move for d in range(3)] for c in range(3)]
            w = wrow * (gauss_weight(r) * float(weights[p])) * (size * size * size)
            q = [None] * 4
            for d, e in pairs:
                d0 = dot3(M, M, d, e)
                d2 = dot3(K, K, d, e)
                if d == e:
                    d0 = d0 - 1.0
                    d1 = 2.0 * dot3(M, K, d, d)
                else:
                    d1 = dot3(M, K, d, e) + dot3(K, M, d, e)
                terms = [2.0 * (d0 * d1), d1 * d1 + 2.0 * (d0 * d2), 2.0 * (d1 * d2), d2 * d2]
                for n in range(4):
                    term = terms[n] if d == e else 2.0 * terms[n]
                    q[n] = term if q[n] is None else q[n] + term
            s1, s2, s3, s4 = s1 + w * q[0], s2 + w * q[1], s3 + w * q[2], s4 + w * q[3]
        return s1, s2, s3, s4

    sums = lax.fori_loop(0, 4 * X, trial, (zero,) * 4)
    block = zero
    for n, part in enumerate((esum, ssum) + tuple(sums)):
        block = jnp.where(row == n, jnp.sum(part, axis=0, keepdims=True), block)
    column = jnp.sum(block, axis=1, keepdims=True)
    column = jnp.where(row == 6, bound, jnp.broadcast_to(column, (ROWS, Z)))
    me = (index[0] * sizes[1] + index[1]) * sizes[2] + index[2]
    groups = RED.shape[2]
    for n in range(groups):
        RED[1, 0, n] = jnp.where(lane + n * Z == me, column, 0.0)
    red_start(1, 0)
    for c in range(3):
        for k in range(3):
            slab[c * NX : (c + 1) * NX, :, k * Z : (k + 1) * Z] = GN[c, 0:NX, k]
    red_finish(1, 0, jnp.add)
    red_start(1, 1)
    woven = lax.dot_general(
        slab[...].reshape(3 * NX * ROWS, 3 * Z), perm[...], (((1,), (1,)), ((), ())),
        precision=lax.Precision.HIGHEST, preferred_element_type=f32,
    ).reshape(3, NX, ROWS, 3 * Z)
    grad[...] = woven[:, :, 0:NY, :]
    for ix in range(X):
        adv[:, ix] = U[:, ix * Y : ix * Y + Y, :]
    red_finish(1, 1, jnp.add)
    every = [RED[1, 2, n] for n in range(groups)]

    def over_all(parts):
        return sum(jnp.sum(x, axis=1, keepdims=True) for x in parts)

    etot = over_all([x[0:1] for x in every])
    stot = over_all([x[1:2] for x in every])
    step = trial_step / jnp.sqrt(1.0 + stot / entries)
    parts = []
    for n, x in enumerate(every):
        own = jnp.where(lane[0:1] + n * Z < devices, x[6:7], 1.0)
        h = step / own
        parts.append(x[0:1] + h * (x[2:3] + h * (x[3:4] + h * (x[4:5] + h * x[5:6]))))
    ttot = over_all(parts)
    l1 = lax.broadcasted_iota(jnp.int32, (1, Z), 1)
    checks[...] = jnp.where(
        l1 == 0, etot / elements, jnp.where(l1 == 1, stot / entries, ttot / elements)
    )


def solution(mesh):
    sizes = tuple(mesh.shape[a] for a in AXES)

    def on_device(displacement, size_field_modes, velocity):
        modes, X, Y, Z = size_field_modes.shape
        assert Y == 2 and displacement.shape == (3, 3 * X, 3 * Y, 3 * Z)
        R, NX, NY = 4 * Y, 3 * X, 3 * Y
        tab = jnp.asarray(row_tables(Y, Z))
        peers = sizes[0] - 1 + sizes[1] * sizes[2] - 1
        groups = -(-sizes[0] * sizes[1] * sizes[2] // Z)
        S = 2 * SUBSTEPS
        vm = lambda *shape: pltpu.VMEM(shape, jnp.float32)
        dma = lambda *shape: pltpu.SemaphoreType.DMA(shape)
        spec = pl.BlockSpec(memory_space=pltpu.VMEM)
        adv, grad, checks = pl.pallas_call(
            functools.partial(kernel, sizes, X, Y, Z),
            out_shape=(
                jax.ShapeDtypeStruct(size_field_modes.shape, jnp.float32),
                jax.ShapeDtypeStruct(displacement.shape, jnp.float32),
                jax.ShapeDtypeStruct((1, Z), jnp.float32),
            ),
            in_specs=[spec] * 4,
            out_specs=(spec,) * 3,
            scratch_shapes=[
                vm(3 * Z, 3 * Z), vm(3 * NX, R, 3 * Z), vm(27, R, Z), vm(27, R, Z), vm(3, R, Z), vm(3, 4, R, Z),
                vm(S, 2, 10, Y, Z), vm(S, 2, 10, Y, Z), vm(S, 2, 10, X, Z), vm(S, 2, 10, X, Z),
                vm(S, 2, R, Z), vm(S, 2, R, Z),
                vm(2, 3, groups, R, Z), vm(2, peers, groups, R, Z),
                vm(3, NX + 1, 4, R, Z), vm(3, NX + 1, 4, R, Z),
                vm(3, 3, NX + 1, 4, R, Z), vm(3, 3, X, 4, 4, R, Z), vm(3, 3, X, 4, 4, R, Z), vm(2, NX + 1, 4, R, Z), vm(X, 4, 4, R, Z), vm(R, Z),
                vm(1, 3, 3, R, Z), vm(1, 3, NX + 1, 3, Z), vm(1, 3, NX + 1, 3, Z), vm(1, R, Z), vm(1, R, Z),
                vm(2, 3, 4, R, Z), vm(2, 3, NX + 1, 4, Z), vm(2, 3, NX + 1, 4, Z), vm(2, R, Z), vm(2, R, Z),
                dma(S, 6), dma(S, 6), dma(2, peers), dma(2, peers), dma(1, 3), dma(1, 3), dma(6), dma(6),
            ],
            compiler_params=pltpu.CompilerParams(collective_id=0, has_side_effects=True),
        )(displacement, size_field_modes, velocity, tab)
        return adv, grad, checks[0, 0:3]

    return jax.shard_map(
        on_device,
        mesh=mesh,
        in_specs=(P(None, "gx", "gy", "gz"),) * 3,
        out_specs=(P(None, "gx", "gy", "gz"), P(None, "gx", "gy", "gz"), P()),
        check_vma=False,
    )
```

time: 72.1 us -> 64.6 us (0.90)
  Pallas kernels: 66.9 us -> 59.4 us
    pallas_call x1, Pallas kernels: 66.9 us -> 59.4 us  [on_device(): pl.pallas_call(functools.partial(kernel, sizes, X, Y, Z), out_shape=(jax....]
where the time goes in v1:
time: 64.6 us; the launch traced here: 64.3 us
  Pallas kernels  59.4 us (92%)
  local copies, waits for them, and re-layouts  4.25 us (7%)
  between operations  0.65 us (1%)
    pallas_call x1, Pallas kernels, on_device(): pl.pallas_call(functools.partial(kernel, sizes, X, Y, Z), out_shape=(jax....  59.4 us
    unnamed x4, local copies, waits for them, and re-layouts  3.74 us

profile of v1, /device:TPU:0, one launch (start us, length us, event | category | flops | bytes accessed | tf_op | source)
XLA Modules:
  0.0 64.3 jit_solution(10414992780537169175)
XLA Ops:
  0.6 59.4 %shard_map.67 = (f32[27,2,2,128]{3,2,1,0:T(2,128)}, f32[3,6,6,384]{3,2,1,0:T(8,128)}, f32[1,128]{1,0:T(1,128)}) custom-call(f32[3,6,6,384]{3,2,1,0:T(8,128)} %disp.1, f32[27,2,2,128]{3,2,1,0:T(2,128)} %modes.1, f32[3,2,2,128]{3,2,1,0:T(2,128)} %vel.1, f32[37,8,128]{2,1,0:T(8,128)} %constant.2.clone.tab), custom_call_target="tpu_custom_call" | custom-call | tf_op jit(solution)/shard_map/pallas_call | solution.py:632
  60.1 0.0 copy-start
  60.1 0.7 %copy-done = f32[1,128]{1,0:T(1,128)S(1)} copy-done((f32[1,128]{1,0:T(1,128)S(1)}, f32[1,128]{1,0:T(1,128)}, u32[]{:S(2)}) %copy-start) | copy-done | bytes 536
  60.8 0.5 slice_bitcast_fusion
  61.3 1.4 %copy.9 = f32[27,2,2,128]{3,2,1,0:T(2,128)} copy(f32[27,2,2,128]{3,2,1,0:T(2,128)} %get-tuple-element.12) | data formatting | bytes 110592
  62.7 1.6 %copy.10 = f32[3,6,6,384]{3,2,1,0:T(8,128)} copy(f32[3,6,6,384]{3,2,1,0:T(8,128)} %get-tuple-element.13) | data formatting | bytes 331776
Async XLA Ops:
  60.1 0.7 %copy-start = (f32[1,128]{1,0:T(1,128)S(1)}, f32[1,128]{1,0:T(1,128)}, u32[]{:S(2)}) copy-start(f32[1,128]{1,0:T(1,128)} %get-tuple-element.8) | copy-start | bytes 1540

commit v2 on v1

--- a/solution.py
+++ b/solution.py
@@ -164,7 +164,7 @@
         off = 0 if phase == 0 else sizes[0] - 1
         copies = red_copies(r, phase)
         for cp in copies:
-            cp.wait()
+            cp.wait_recv()
         total = RED[r, phase]
         for n in range(len(copies)):
             total = op(total, REDR[r, off + n])
@@ -283,7 +283,7 @@
         between()
         for d in range(3):
             for cp in halo_copies(s, (d,)):
-                cp.wait()
+                cp.wait_recv()
             if first:
                 high = v[d] + next_of(d, v[d], s, 9)
                 lowf = prev_of(d, v[d], s, 9) + v[d]
@@ -609,6 +609,13 @@
         h = step / own
         parts.append(x[0:1] + h * (x[2:3] + h * (x[3:4] + h * (x[4:5] + h * x[5:6]))))
     ttot = over_all(parts)
+    for t in range(2 * SUBSTEPS):
+        for cp in halo_copies(t, (0, 1, 2)):
+            cp.wait_send()
+    for r in range(2):
+        for phase in range(2):
+            for cp in red_copies(r, phase):
+                cp.wait_send()
     l1 = lax.broadcasted_iota(jnp.int32, (1, Z), 1)
     checks[...] = jnp.where(
         l1 == 0, etot / elements, jnp.where(l1 == 1, stot / entries, ttot / elements)

time: 64.6 us -> 64.2 us (level)
  no operation moved by 1% of the time
where the time goes in v2:
time: 64.2 us; the launch traced here: 64 us
  Pallas kernels  59.1 us (92%)
  local copies, waits for them, and re-layouts  4.25 us (7%)
  between operations  0.65 us (1%)
    pallas_call x1, Pallas kernels, on_device(): pl.pallas_call(functools.partial(kernel, sizes, X, Y, Z), out_shape=(jax....  59.1 us
    unnamed x4, local copies, waits for them, and re-layouts  3.74 us

profile of v2, /device:TPU:0, one launch (start us, length us, event | category | flops | bytes accessed | tf_op | source)
XLA Modules:
  0.0 64.0 jit_solution(1686484482816151590)
XLA Ops:
  0.6 59.1 %shard_map.67 = (f32[27,2,2,128]{3,2,1,0:T(2,128)}, f32[3,6,6,384]{3,2,1,0:T(8,128)}, f32[1,128]{1,0:T(1,128)}) custom-call(f32[3,6,6,384]{3,2,1,0:T(8,128)} %disp.1, f32[27,2,2,128]{3,2,1,0:T(2,128)} %modes.1, f32[3,2,2,128]{3,2,1,0:T(2,128)} %vel.1, f32[37,8,128]{2,1,0:T(8,128)} %constant.2.clone.tab), custom_call_target="tpu_custom_call" | custom-call | tf_op jit(solution)/shard_map/pallas_call | solution.py:639
  59.8 0.0 copy-start
  59.8 0.7 %copy-done = f32[1,128]{1,0:T(1,128)S(1)} copy-done((f32[1,128]{1,0:T(1,128)S(1)}, f32[1,128]{1,0:T(1,128)}, u32[]{:S(2)}) %copy-start) | copy-done | bytes 536
  60.4 0.5 slice_bitcast_fusion
  60.9 1.4 %copy.9 = f32[27,2,2,128]{3,2,1,0:T(2,128)} copy(f32[27,2,2,128]{3,2,1,0:T(2,128)} %get-tuple-element.12) | data formatting | bytes 110592
  62.4 1.6 %copy.10 = f32[3,6,6,384]{3,2,1,0:T(8,128)} copy(f32[3,6,6,384]{3,2,1,0:T(8,128)} %get-tuple-element.13) | data formatting | bytes 331776
Async XLA Ops:
  59.8 0.7 %copy-start = (f32[1,128]{1,0:T(1,128)S(1)}, f32[1,128]{1,0:T(1,128)}, u32[]{:S(2)}) copy-start(f32[1,128]{1,0:T(1,128)} %get-tuple-element.8) | copy-start | bytes 1540
